TPU v7x, 256 devices: a whole 4x4x8 slice. The times are simulated.
256 devices in a mesh: dp: 16 (over z, core), row: 4 (over y), col: 4 (over x).
Axes of the slice: x: 4, y: 4, z: 8, core: 2. Of those that a mesh axis runs over, the one named last changes fastest.
Arguments:
- grad_up: bfloat16 [16, 2048, 8192], P('dp', 'col', 'row'), may hold values from -24 to 24
- grad_down: bfloat16 [16, 8192, 2048], P('dp', 'row', 'col'), may hold values from -24 to 24
- master_up: float32 [2048, 8192], P('col', ('row', 'dp')), may hold values from -6 to 6
- moment_up: float32 [2048, 8192], P('col', ('row', 'dp')), may hold values from -3 to 3
- second_up: float32 [2048, 8192], P('col', ('row', 'dp')), may hold values from 0.01 to 1
- master_down: float32 [8192, 2048], P(('row', 'dp'), 'col'), may hold values from -6 to 6
- moment_down: float32 [8192, 2048], P(('row', 'dp'), 'col'), may hold values from -3 to 3
- second_down: float32 [8192, 2048], P(('row', 'dp'), 'col'), may hold values from 0.01 to 1
Outputs:
- new_master_up: float32 [2048, 8192], P('col', ('row', 'dp'))
- new_moment_up: float32 [2048, 8192], P('col', ('row', 'dp'))
- new_second_up: float32 [2048, 8192], P('col', ('row', 'dp'))
- new_master_down: float32 [8192, 2048], P(('row', 'dp'), 'col')
- new_moment_down: float32 [8192, 2048], P(('row', 'dp'), 'col')
- new_second_down: float32 [8192, 2048], P(('row', 'dp'), 'col')
- weight_up: bfloat16 [2048, 8192], P('col', 'row')
- weight_down: bfloat16 [8192, 2048], P('row', 'col')
All inputs are finite; a program needn't handle non-finite values.
Results may differ from a plain program's by a relative error of at most 0.012.
Values may be sent and summed in bfloat16 or wider, within the bound.
A program may use at most 64 MiB of HBM per device.

v0:
```python
import jax
import jax.numpy as jnp
from jax import lax
from jax.sharding import PartitionSpec as P

D = 2048
STEP = 10


def in_blocks(value, dim, length):
    before, after = (value.shape[:dim], value.shape[dim + 1 :])
    return jnp.moveaxis(value.reshape(*before, length, -1, *after), dim, 0)


def one_scatter(arrays, axis, dims):
    length = lax.axis_size(axis)
    blocks = [in_blocks(a, dim, length) for a, dim in zip(arrays, dims)]
    lines = jnp.concatenate([b.reshape(length, -1) for b in blocks], axis=1)
    rows = max(16, -(-lines.shape[1] // 1024) * 8)
    lines = jnp.pad(lines, ((0, 0), (0, rows * 128 - lines.shape[1]))).reshape(-1, 128)
    line, at, gathered = (lax.psum_scatter(lines, axis, tiled=True).reshape(-1), 0, [])
    for b in blocks:
        part = b[0]
        gathered.append(line[at : at + part.size].reshape(part.shape))
        at += part.size
    return tuple(gathered)


def from_everyone(value, axis):
    copies = jnp.broadcast_to(value, (lax.axis_size(axis), *value.shape))
    return lax.all_to_all(copies, axis, split_axis=0, concat_axis=0, tiled=True)


def over_copies(value, axis):
    return from_everyone(value, axis).sum(axis=0)


def in_one(arrays, axis):
    line, at, gathered = (jnp.concatenate([a.reshape(-1) for a in arrays]), 0, [])
    so_far = over_copies(line, axis)
    for a in arrays:
        gathered.append(so_far[at : at + a.size].reshape(a.shape))
        at += a.size
    return tuple(gathered)


def gather_turned(arrays, axis, dims):
    turned = [jnp.moveaxis(a, dim, 0) for a, dim in zip(arrays, dims)]
    widths = [t[0].size for t in turned]
    both = jnp.concatenate([t.reshape(-1, w) for t, w in zip(turned, widths)], axis=1)
    filled = lax.all_gather(both, axis, axis=0, tiled=True)
    blocks = jnp.split(filled, [sum(widths[:k]) for k in range(1, len(widths))], axis=1)
    return tuple(
        (
            jnp.moveaxis(b.reshape(-1, *t.shape[1:]), 0, dim)
            for b, t, dim in zip(blocks, turned, dims)
        )
    )


def adam_move(master, moment, second, grad):
    new_moment = 0.9 * moment + 0.1 * grad
    new_second = 0.95 * second + 0.05 * grad * grad
    first_hat = new_moment / (1.0 - 0.9**STEP)
    second_hat = new_second / (1.0 - 0.95**STEP)
    moved = master - 0.2 * first_hat / (jnp.sqrt(second_hat) + 1e-08)
    return (moved, new_moment, new_second)


def on_device(
    grad_up, grad_down, master_up, moment_up, second_up, master_down, moment_down, second_down
):
    summed_up, summed_down = tuple(
        (
            part.astype(jnp.float32)
            for part in one_scatter(
                (
                    grad_up[0].astype(jnp.float32).astype(jnp.bfloat16),
                    grad_down[0].astype(jnp.float32).astype(jnp.bfloat16),
                ),
                "dp",
                (1, 0),
            )
        )
    )
    factor = 1.0 / lax.axis_size("dp")
    moved_up, mom_up, sec_up = adam_move(master_up, moment_up, second_up, summed_up * factor)
    moved_down, mom_down, sec_down = adam_move(
        master_down, moment_down, second_down, summed_down * factor
    )
    squares_up = jnp.sum(moved_up * moved_up, axis=0)
    squares_down = jnp.sum(moved_down * moved_down, axis=1)
    squares_up, squares_down = in_one((squares_up, squares_down), "col")
    norm_up = moved_up * lax.rsqrt(squares_up / D + 1e-06)[None, :]
    norm_down = moved_down * lax.rsqrt(squares_down / D + 1e-06)[:, None]
    weight_up, weight_down = gather_turned(
        (norm_up.astype(jnp.bfloat16), norm_down.astype(jnp.bfloat16)), "dp", (1, 0)
    )
    return (norm_up, mom_up, sec_up, norm_down, mom_down, sec_down, weight_up, weight_down)


def solution(mesh):
    return jax.shard_map(
        on_device,
        mesh=mesh,
        in_specs=(
            P("dp", "col", "row"),
            P("dp", "row", "col"),
            P("col", ("row", "dp")),
            P("col", ("row", "dp")),
            P("col", ("row", "dp")),
            P(("row", "dp"), "col"),
            P(("row", "dp"), "col"),
            P(("row", "dp"), "col"),
        ),
        out_specs=(
            P("col", ("row", "dp")),
            P("col", ("row", "dp")),
            P("col", ("row", "dp")),
            P(("row", "dp"), "col"),
            P(("row", "dp"), "col"),
            P(("row", "dp"), "col"),
            P("col", "row"),
            P("row", "col"),
        ),
        check_vma=False,
    )
```

profile of v0, /device:TPU:1, one launch (start us, length us, event | category | flops | bytes accessed | tf_op | source)
XLA Modules:
  0.0 154.9 jit_solution(15130753836143395686)
XLA Ops:
  7.2 0.0 reduce-scatter.2.cloned.1.call-start
  7.2 2.2 %copy.30 = bf16[64,8,16,128]{3,2,1,0:T(8,128)(2,1)S(1)} copy(bf16[64,8,16,128]{3,1,2,0:T(8,128)(2,1)} %bitcast.16) | data formatting | bytes 4194304
  9.4 0.1 copy.32
  9.6 3.2 %reshape_reshape.3 = bf16[16,65536]{1,0:T(8,128)(2,1)} reshape(bf16[1,2048,512]{2,1,0:T(8,128)(2,1)} %param.9) | data formatting | bytes 4194304 | tf_op jit(solution)/shard_map/reshape;reshape | solution.py:18
  12.7 3.8 %pad_maximum_fusion = bf16[16,131072]{1,0:T(8,128)(2,1)} fusion(bf16[16,65536]{1,0:T(8,128)(2,1)} %reshape_reshape.3, bf16[16,65536]{1,0:T(8,128)(2,1)S(1)} %bitcast.15), kind=kLoop, calls=%fused_computation | loop fusion | flops 8388608 | bytes 8388608 | tf_op jit(solution)/shard_map/concatenate | solution.py:18
  16.6 4.8 %reshape.50 = bf16[16384,128]{1,0:T(8,128)(2,1)} reshape(bf16[16,131072]{1,0:T(8,128)(2,1)} %pad_maximum_fusion) | data formatting | bytes 8388608 | tf_op jit(solution)/shard_map/reshape | solution.py:20
  21.4 0.0 copy-start.1
  21.4 0.0 copy-start.2
  21.4 0.0 copy-start.3
  21.4 0.0 reduce-scatter.2.cloned.1.call-update
  21.4 0.0 copy-start.4
  21.4 0.0 copy-start.5
  21.4 0.0 copy-start.6
  21.5 0.0 all-gather.2.cloned.1.call-start
  21.5 64.1 %reduce-scatter.2.cloned.1.call-done = bf16[1024,128]{1,0:T(8,128)(2,1)} async-done(((bf16[16384,128]{1,0:T(8,128)(2,1)}), bf16[1024,128]{1,0:T(8,128)(2,1)}) %reduce-scatter.2.cloned.1.call-update) | async-done | bytes 262160 | tf_op jit(solution)/shard_map/reduce_scatter | solution.py:21
  85.6 0.0 copy-done.1
  85.6 0.0 copy-done.2
  85.6 0.0 copy-done.3
  85.6 2.0 %fusion.3 = (f32[512,128]{1,0:T(8,128)S(1)}, f32[512,128]{1,0:T(8,128)S(1)}, f32[128]{0:T(128)S(1)}, f32[512,128]{1,0:T(8,128)S(1)}, f32[512,128]{1,0:T(8,128)}, /*index=5*/f32[512,128]{1,0:T(8,128)}) fusion(bf16[1024,128]{1,0:T(8,128)(2,1)} %reduce-scatter.2.cloned.1.call-done, f32[512,128]{1,0:T(8,128)S(1)} %copy-done.1, f32[512,128]{1,0:T(8,128)S(1)} %copy-done.2, ...), kind=kLoop, calls=%fused_computation.12 | loop fusion | flops 1376128 | bytes 2359808 | tf_op jit(solution)/shard_map/mul | solution.py:63
  87.7 0.0 copy-done.4
  87.7 0.0 copy-done.5
  87.7 0.0 copy-done.6
  87.7 0.9 multiply_reduce_fusion
  88.7 7.8 %all_to_all.6 = f32[4,1,256]{2,1,0:T(1,128)S(1)} all-to-all(f32[4,1,256]{2,1,0:T(1,128)S(1)} %broadcast_in_dim.2), channel_id=1, replica_groups=mesh['dp'=16,'row'=4,'col'=4] {'col'}, dimensions={0} | all-to-all | bytes 8192 | tf_op jit(solution)/shard_map/all_to_all | solution.py:31
  96.5 0.0 copy-start
  96.5 0.1 copy.24
  96.6 0.8 fusion.4
  97.4 0.7 pad_maximum_fusion.1
  98.2 0.0 all-gather.2.cloned.1.call-update
  98.2 43.7 %all-gather.2.cloned.1.call-done = bf16[2048,1024]{1,0:T(8,128)(2,1)} async-done(((bf16[128,1024]{1,0:T(8,128)(2,1)}), bf16[2048,1024]{1,0:T(8,128)(2,1)}) %all-gather.2.cloned.1.call-update) | async-done | bytes 4194320 | tf_op jit(solution)/shard_map/all_gather | solution.py:51
  141.9 3.8 %fusion.7 = (bf16[2048,512]{1,0:T(8,128)(2,1)}, bf16[512,2048]{0,1:T(8,128)(2,1)S(1)}) fusion(bf16[2048,1024]{1,0:T(8,128)(2,1)} %all-gather.2.cloned.1.call-done), kind=kLoop, calls=%fused_computation.27 | loop fusion | bytes 8388608 | tf_op jit(solution)/shard_map/split | solution.py:52
  145.7 0.0 copy-done
  145.7 2.4 %copy.25 = bf16[512,2048]{1,0:T(8,128)(2,1)} copy(bf16[512,2048]{0,1:T(8,128)(2,1)S(1)} %get-tuple-element.43) | data formatting | bytes 4194304
  (7 shorter events, 0.2 us)
Async XLA Ops:
  7.2 78.4 %reduce-scatter.2.cloned.1.call-start = ((), (), s32[]{:S(2)}) async-start(), calls=%async_computation.2 | async-start | bytes 4456448 | tf_op jit(solution)/shard_map/reduce_scatter | solution.py:21
  21.4 64.2 %copy-start.1 = (f32[512,128]{1,0:T(8,128)S(1)}, f32[512,128]{1,0:T(8,128)}, u32[]{:S(2)}) copy-start(f32[512,128]{1,0:T(8,128)} %param.10) | copy-start | bytes 786436
  21.4 64.2 %copy-start.2 = (f32[512,128]{1,0:T(8,128)S(1)}, f32[512,128]{1,0:T(8,128)}, u32[]{:S(2)}) copy-start(f32[512,128]{1,0:T(8,128)} %param.12) | copy-start | bytes 786436
  21.4 64.2 %copy-start.3 = (f32[512,128]{1,0:T(8,128)S(1)}, f32[512,128]{1,0:T(8,128)}, u32[]{:S(2)}) copy-start(f32[512,128]{1,0:T(8,128)} %param.11) | copy-start | bytes 786436
  21.4 66.3 %copy-start.4 = (f32[128,512]{1,0:T(8,128)S(1)}, f32[128,512]{1,0:T(8,128)}, u32[]{:S(2)}) copy-start(f32[128,512]{1,0:T(8,128)} %param.13) | copy-start | bytes 786436
  21.4 66.3 %copy-start.5 = (f32[128,512]{1,0:T(8,128)S(1)}, f32[128,512]{1,0:T(8,128)}, u32[]{:S(2)}) copy-start(f32[128,512]{1,0:T(8,128)} %param.14) | copy-start | bytes 786436
  21.4 66.3 %copy-start.6 = (f32[128,512]{1,0:T(8,128)S(1)}, f32[128,512]{1,0:T(8,128)}, u32[]{:S(2)}) copy-start(f32[128,512]{1,0:T(8,128)} %param.15) | copy-start | bytes 786436
  21.5 120.5 %all-gather.2.cloned.1.call-start = ((), (), s32[]{:S(2)}) async-start(), calls=%async_computation.3 | async-start | bytes 4456448 | tf_op jit(solution)/shard_map/all_gather | solution.py:51
  96.5 49.2 %copy-start = (f32[512,128]{1,0:T(8,128)}, f32[512,128]{1,0:T(8,128)S(1)}, u32[]{:S(2)}) copy-start(f32[512,128]{1,0:T(8,128)S(1)} %broadcast_multiply_fusion.1) | copy-start | bytes 786436
Sparse Core Ops, SparseCore 0:
  21.5 63.9 reduce-scatter.1
  98.3 43.5 all-gather.1
where the time goes:
time: 155 us
  waiting for transfers between devices  108 us (70%)
  local copies, waits for them, and re-layouts  16.7 us (11%)
  between operations  14.2 us (9%)
  other arithmetic  8.37 us (5%)
  blocking collectives  7.77 us (5%)
    reduce_scatter x1, waiting for transfers between devices, one_scatter(): lax.psum_scatter(lines, axis, tiled=True).reshape(-1)  64.1 us
    all_gather x1, waiting for transfers between devices, gather_turned(): filled = lax.all_gather(both, axis, axis=0, tiled=True)  43.7 us
    all_to_all x1, blocking collectives, from_everyone(): return lax.all_to_all(copies, axis, split_axis=0, concat_axis=0, tiled=True)  7.77 us
    reshape x1, local copies, waits for them, and re-layouts, one_scatter(): jnp.pad(lines, ((0, 0), (0, rows * 128 - lines.shape[1]))).reshape(-1, 128)  4.81 us
    unnamed x16, local copies, waits for them, and re-layouts  4.6 us
    concatenate x1, other arithmetic, one_scatter(): lines = jnp.concatenate([b.reshape(length, -1) for b in blocks], axis=1)  3.83 us
    split x1, local copies, waits for them, and re-layouts, gather_turned(): jnp.split(filled, [sum(widths[:k]) for k in range(1, len(widths))], axis=1)  3.81 us
    another operation x1, local copies, waits for them, and re-layouts, one_scatter(): lines = jnp.concatenate([b.reshape(length, -1) for b in blocks], axis=1)  3.17 us
  transfers between devices with their start and end apart: 2, of which 2 were waited for; matrix products, arithmetic and copies ran while one was open for 0% of the time, Pallas kernels for 0%

commit v1 on v0

v1 whole, which is shorter than its diff:
```python
import jax
import jax.numpy as jnp
from jax import lax
from jax.experimental import pallas as pl
from jax.experimental.pallas import tpu as pltpu
from jax.sharding import PartitionSpec as P

D = 2048
STEP = 10
MESH = pl.DeviceIdType.MESH
F32, BF16 = jnp.float32, jnp.bfloat16
NZ = 8
S = 2
UP, DOWN = 0, 1
RIGHT, LEFT = 0, 1
A, B = 0, 1
BLOCK = ((512, 128), (128, 512))
PIECE = tuple((r // (2 * S), c) for r, c in BLOCK)
OPT = ((512, 128), (128, 512))


def adam_move(master, moment, second, grad):
    new_moment = 0.9 * moment + 0.1 * grad
    new_second = 0.95 * second + 0.05 * grad * grad
    first_hat = new_moment / (1.0 - 0.9**STEP)
    second_hat = new_second / (1.0 - 0.95**STEP)
    moved = master - 0.2 * first_hat / (jnp.sqrt(second_hat) + 1e-08)
    return (moved, new_moment, new_second)


def reaches(way, half, hop):
    return hop <= 3 or (hop == 4 and half == way)


def step_kernel(*refs):
    grads, state = refs[:2], (refs[2:5], refs[5:8])
    outs = (refs[8:11], refs[11:14])
    weights = refs[14:16]
    it = iter(refs[16:])
    own, par = (next(it), next(it)), (next(it), next(it))
    snd, rcv = (next(it), next(it)), (next(it), next(it))
    held = (tuple(next(it) for _ in range(3)), tuple(next(it) for _ in range(3)))
    ex_s, ex_r, sq, scale = next(it), next(it), next(it), next(it)
    own_sem, state_sem = next(it), next(it)
    par_ss, par_rs = next(it), next(it)
    rs_ss, rs_rs = next(it), next(it)
    ag_ss, ag_rs = next(it), next(it)
    cp_ss, cp_rs = next(it), next(it)
    ex_ss, ex_rs = next(it), next(it)

    dp, row, col = lax.axis_index("dp"), lax.axis_index("row"), lax.axis_index("col")
    z, core = dp // 2, dp % 2
    partner = (z * 2 + (1 - core), row, col)
    beside = (
        (lax.rem(dp + 2, 2 * NZ), row, col),
        (lax.rem(dp + 2 * NZ - 2, 2 * NZ), row, col),
    )
    peers = tuple((dp, row, lax.rem(col + j, 4)) for j in (1, 2, 3))

    def block_at(r, parity):
        return lax.rem(z + r, NZ) * 2 + parity

    def grad_block(t, r, parity):
        at = pl.multiple_of(block_at(r, parity) * 128, 128)
        if t == UP:
            return grads[t].at[0, :, pl.ds(at, 128)]
        return grads[t].at[0, pl.ds(at, 128), :]

    order = (4, 3, 5, 2, 6, 1, 7, 0)
    own_cp, par_cp = {}, {}
    for r in order:
        for t in (UP, DOWN):
            own_cp[t, r] = pltpu.make_async_copy(
                grad_block(t, r, core), own[t].at[r], own_sem.at[t, r]
            )
            own_cp[t, r].start()
    state_cp = {}
    for t in (UP, DOWN):
        for k in range(3):
            state_cp[t, k] = pltpu.make_async_copy(state[t][k], held[t][k], state_sem.at[t, k])
            state_cp[t, k].start()

    barrier = pltpu.get_barrier_semaphore()
    for device in (partner, *beside, *peers):
        pl.semaphore_signal(barrier, inc=1, device_id=device, device_id_type=MESH)
    pl.semaphore_wait(barrier, 6)

    sent = []

    def send(src, dst, ss, rs, to):
        copy = pltpu.make_async_remote_copy(
            src_ref=src, dst_ref=dst, send_sem=ss, recv_sem=rs, device_id=to, device_id_type=MESH
        )
        copy.start()
        sent.append(copy)
        return copy

    for r in order:
        for t in (UP, DOWN):
            par_cp[t, r] = send(
                grad_block(t, r, 1 - core), par[t].at[r], par_ss.at[t, r], par_rs.at[t, r], partner
            )

    def rows_of(t, half, s):
        n = PIECE[t][0]
        return pl.ds((half * S + s) * n, n)

    ready = set()

    def chip_sum(t, r, half, s):
        if (t, r) not in ready:
            ready.add((t, r))
            own_cp[t, r].wait()
            par_cp[t, r].wait_recv()
        at = rows_of(t, half, s)
        return own[t][r, at, :].astype(F32) + par[t][r, at, :].astype(F32)

    rs_cp = {}

    def reduce_hop(t, way, half, hop, s):
        total = chip_sum(t, hop if way == RIGHT else NZ - hop, half, s)
        if reaches(way, half, hop + 1):
            rs_cp[t, way, half, hop + 1, s].wait_recv()
            total += rcv[t][way, half, hop, s].astype(F32)
        snd[t][way, half, hop - 1, s] = total.astype(BF16)
        rs_cp[t, way, half, hop, s] = send(
            snd[t].at[way, half, hop - 1, s],
            rcv[t].at[way, half, hop - 1, s],
            rs_ss.at[t, way, half, hop - 1, s],
            rs_rs.at[t, way, half, hop - 1, s],
            beside[way],
        )

    def reduce_pair(t, which):
        hop, far = which
        for s in range(S):
            for way in (RIGHT, LEFT):
                reduce_hop(t, way, way if far else 1 - way, hop, s)

    ex_cp = {}

    def finish_sum(t):
        for k in range(3):
            state_cp[t, k].wait()
        acc = jnp.zeros((8, 128), F32)
        for half in (A, B):
            for s in range(S):
                base = chip_sum(t, 0, half, s)
                n = PIECE[t][0]
                for way in (RIGHT, LEFT):
                    rs_cp[t, way, half, 1, s].wait_recv()
                step = n // 2
                for i in range(0, n, step):
                    at = pl.ds((half * S + s) * n + i, step)
                    grad = own[t][0, at, :].astype(F32) + par[t][0, at, :].astype(F32)
                    for way in (RIGHT, LEFT):
                        grad += rcv[t][way, half, 0, s, pl.ds(i, step), :].astype(F32)
                    moved, mom, sec = adam_move(
                        held[t][0][at, :], held[t][1][at, :], held[t][2][at, :], grad * (1.0 / 16.0)
                    )
                    outs[t][0][at, :] = moved
                    outs[t][1][at, :] = mom
                    outs[t][2][at, :] = sec
                    square = moved * moved
                    if t == UP:
                        acc += square.reshape(step // 8, 8, 128).sum(axis=0)
                    else:
                        sq[at, :] = (
                            square[:, 0:128]
                            + square[:, 128:256]
                            + square[:, 256:384]
                            + square[:, 384:512]
                        )
        if t == DOWN:
            acc = sq[...].T.reshape(16, 8, 128).sum(axis=0)
        ex_s[t] = acc
        for j, peer in enumerate(peers):
            ex_cp[t, j] = send(ex_s.at[t], ex_r.at[t, j], ex_ss.at[t, j], ex_rs.at[t, j], peer)

    def slot(t, owner, half, s):
        n = PIECE[t][0]
        if t == UP:
            return weights[t].at[owner, rows_of(t, half, s), :]
        return weights[t].at[pl.ds(pl.multiple_of(owner * 128 + (half * S + s) * n, n), n), :]

    def renormalize(t):
        for j in range(3):
            ex_cp[t, j].wait_recv()
        total = ex_s[t] + ex_r[t, 0] + ex_r[t, 1] + ex_r[t, 2]
        factor = lax.rsqrt(total.sum(axis=0, keepdims=True) / D + 1e-06)
        rows = OPT[t][0]
        if t == UP:
            for i in range(0, rows, 64):
                norm = outs[t][0][pl.ds(i, 64), :] * factor
                outs[t][0][pl.ds(i, 64), :] = norm
                weights[t][dp, pl.ds(i, 64), :] = norm.astype(BF16)
        else:
            scale[...] = jnp.broadcast_to(factor, (128, 128)).T
            at0 = pl.multiple_of(dp * 128, 128)
            for i in range(0, rows, 16):
                f = scale[pl.ds(i, 16), :]
                norm = outs[t][0][pl.ds(i, 16), :] * jnp.concatenate([f, f, f, f], axis=1)
                outs[t][0][pl.ds(i, 16), :] = norm
                weights[t][pl.ds(pl.multiple_of(at0 + i, 16), 16), :] = norm.astype(BF16)

    ag_cp, copies = {}, []

    def to_partner(t, owner, half, s, n):
        at = slot(t, owner, half, s)
        copies.append(send(at, at, cp_ss.at[t, n, s], cp_rs.at[t, n, s], partner))

    def gather_hop(t, way, half, hop, s):
        back = NZ - (hop - 1) if way == RIGHT else hop - 1
        owner = block_at(back, core)
        at = slot(t, owner, half, s)
        if hop > 1:
            ag_cp[t, way, half, hop - 1, s].wait_recv()
        if reaches(way, half, hop):
            ag_cp[t, way, half, hop, s] = send(
                at,
                at,
                ag_ss.at[t, way, half, hop - 1, s],
                ag_rs.at[t, way, half, hop - 1, s],
                beside[way],
            )
        if hop > 1:
            n = 2 + (way * 2 + half) * 4 + hop - 2
            to_partner(t, owner, half, s, n)

    def gather_level(t, hop):
        for half in (0, 1):
            for s in range(S):
                for way in (RIGHT, LEFT):
                    h = way if half == 0 else 1 - way
                    if hop == 1 or reaches(way, h, hop - 1):
                        gather_hop(t, way, h, hop, s)
        if hop == 1:
            for half in (A, B):
                for s in range(S):
                    to_partner(t, dp, half, s, half)

    far, near = True, False
    for t, hop, side in (
        (UP, 4, far),
        (UP, 3, near),
        (DOWN, 4, far),
        (UP, 3, far),
        (UP, 2, near),
        (DOWN, 3, near),
        (UP, 2, far),
        (UP, 1, near),
        (DOWN, 3, far),
        (UP, 1, far),
        (DOWN, 2, near),
        (DOWN, 2, far),
    ):
        reduce_pair(t, (hop, side))
    finish_sum(UP)
    reduce_pair(DOWN, (1, near))
    reduce_pair(DOWN, (1, far))
    renormalize(UP)
    gather_level(UP, 1)
    finish_sum(DOWN)
    gather_level(UP, 2)
    renormalize(DOWN)
    gather_level(DOWN, 1)
    gather_level(UP, 3)
    gather_level(DOWN, 2)
    gather_level(UP, 4)
    gather_level(DOWN, 3)
    gather_level(UP, 5)
    gather_level(DOWN, 4)
    gather_level(DOWN, 5)
    for copy in copies:
        copy.wait_recv()
    for copy in sent:
        copy.wait_send()


def write_kernel(*refs):
    ins, outs, sem = refs[:8], refs[8:16], refs[16]
    copies = []
    for k in range(16):
        copies.append((ins[6].at[k], outs[6].at[:, pl.ds(k * 128, 128)]))
    copies.append((ins[7], outs[7]))
    copies += [(ins[k], outs[k]) for k in range(6)]
    copies = [pltpu.make_async_copy(a, b, sem.at[i]) for i, (a, b) in enumerate(copies)]
    for copy in copies:
        copy.start()
    for copy in copies:
        copy.wait()


def on_device(*args):
    any_space = pl.BlockSpec(memory_space=pltpu.HBM)
    vmem = pl.BlockSpec(memory_space=pltpu.VMEM)
    opt = [(shape, F32) for shape in OPT for _ in range(3)]
    mid = opt + [((2 * NZ, 512, 128), BF16), ((2048, 512), BF16)]
    out = opt + [((512, 2048), BF16), ((2048, 512), BF16)]
    dma = pltpu.SemaphoreType.DMA
    scratch = (
        [pltpu.VMEM((NZ, *BLOCK[t]), BF16) for t in (UP, DOWN)]
        + [pltpu.VMEM((NZ, *BLOCK[t]), BF16) for t in (UP, DOWN)]
        + [pltpu.VMEM((2, 2, 4, S, *PIECE[t]), BF16) for t in (UP, DOWN)]
        + [pltpu.VMEM((2, 2, 4, S, *PIECE[t]), BF16) for t in (UP, DOWN)]
        + [pltpu.VMEM(OPT[t], F32) for t in (UP, DOWN) for _ in range(3)]
        + [
            pltpu.VMEM((2, 8, 128), F32),
            pltpu.VMEM((2, 3, 8, 128), F32),
            pltpu.VMEM((128, 128), F32),
            pltpu.VMEM((128, 128), F32),
            dma((2, NZ)),
            dma((2, 3)),
            dma((2, NZ)),
            dma((2, NZ)),
            dma((2, 2, 2, 4, S)),
            dma((2, 2, 2, 4, S)),
            dma((2, 2, 2, 4, S)),
            dma((2, 2, 2, 4, S)),
            dma((2, 18, S)),
            dma((2, 18, S)),
            dma((2, 3)),
            dma((2, 3)),
        ]
    )
    mids = pl.pallas_call(
        step_kernel,
        out_shape=[pltpu.VMEM(shape, kind) for shape, kind in mid],
        in_specs=[any_space] * 8,
        out_specs=[vmem] * 8,
        scratch_shapes=scratch,
        compiler_params=pltpu.CompilerParams(
            collective_id=0, has_side_effects=True, vmem_limit_bytes=61_000_000
        ),
        name="step",
    )(*args)
    return tuple(
        pl.pallas_call(
            write_kernel,
            out_shape=[jax.ShapeDtypeStruct(shape, kind) for shape, kind in out],
            in_specs=[vmem] * 8,
            out_specs=[pl.BlockSpec(memory_space=pl.ANY)] * 8,
            scratch_shapes=[dma((23,))],
            compiler_params=pltpu.CompilerParams(vmem_limit_bytes=20 * 2**20),
            name="write",
        )(*mids)
    )


def solution(mesh):
    up, down = P("col", ("row", "dp")), P(("row", "dp"), "col")
    return jax.shard_map(
        on_device,
        mesh=mesh,
        in_specs=(P("dp", "col", "row"), P("dp", "row", "col"), up, up, up, down, down, down),
        out_specs=(up, up, up, down, down, down, P("col", "row"), P("row", "col")),
        check_vma=False,
    )
```

time: 155 us -> 62.5 us (0.40)
  waiting for transfers between devices: 108 us -> 0 us
  Pallas kernels: 0 us -> 61.7 us
  local copies, waits for them, and re-layouts: 16.7 us -> 0 us
  between operations: 14.2 us -> 0.64 us
  other arithmetic: 8.37 us -> 0 us
  blocking collectives: 7.77 us -> 0 us
    reduce_scatter x1 -> x0, waiting for transfers between devices: 64.1 us -> none  [one_scatter(): lax.psum_scatter(lines, axis, tiled=True).reshape(-1)]
    pallas_call x0 -> x2, Pallas kernels: none -> 61.7 us  [the longest x1 59.1 us: on_device(): pl.pallas_call(step_kernel, out_shape=[pltpu.VMEM(shape, kind) for shape,...]
    all_gather x1 -> x0, waiting for transfers between devices: 43.7 us -> none  [gather_turned(): filled = lax.all_gather(both, axis, axis=0, tiled=True)]
    all_to_all x1 -> x0, blocking collectives: 7.77 us -> none  [from_everyone(): return lax.all_to_all(copies, axis, split_axis=0, concat_axis=0, tiled=True)]
    reshape x2 -> x0, local copies, waits for them, and re-layouts: 4.95 us -> none  [the longest x1 4.81 us: one_scatter(): jnp.pad(lines, ((0, 0), (0, rows * 128 - lines.shape[1]))).reshape(-1, 128)]
    unnamed x16 -> x0, local copies, waits for them, and re-layouts: 4.6 us -> none
    concatenate x3 -> x0, other arithmetic: 4.57 us -> none  [the longest x1 3.83 us: one_scatter(): lines = jnp.concatenate([b.reshape(length, -1) for b in blocks], axis=1)]
    split x1 -> x0, local copies, waits for them, and re-layouts: 3.81 us -> none  [gather_turned(): jnp.split(filled, [sum(widths[:k]) for k in range(1, len(widths))], axis=1)]
  transfers between devices with their start and end apart: 2 -> 0, of which waited for: 2 -> 0; matrix products, arithmetic and copies ran while one was open for 0% -> 0% of each run, Pallas kernels for 0% -> 0%
where the time goes in v1:
time: 62.5 us; the launch traced here: 62.4 us
  Pallas kernels  61.7 us (99%)
  between operations  0.64 us (1%)
    pallas_call x1, Pallas kernels, on_device(): pl.pallas_call(step_kernel, out_shape=[pltpu.VMEM(shape, kind) for shape,...  59.1 us
    pallas_call x1, Pallas kernels, on_device(): pl.pallas_call(write_kernel, out_shape=[jax.ShapeDtypeStruct(shape, kind)...  2.68 us

profile of v1, /device:TPU:1, one launch (start us, length us, event | category | flops | bytes accessed | tf_op | source)
XLA Modules:
  0.0 62.4 jit_solution(1937539579900126054)
XLA Ops:
  0.6 59.1 %step.1 = (f32[512,128]{1,0:T(8,128)S(1)}, f32[512,128]{1,0:T(8,128)S(1)}, f32[512,128]{1,0:T(8,128)S(1)}, f32[128,512]{1,0:T(8,128)S(1)}, f32[128,512]{1,0:T(8,...) custom-call(bf16[1,512,2048]{2,1,0:T(8,128)(2,1)} %refs_0_.1, ...), custom_call_target="tpu_custom_call" | custom-call | tf_op jit(solution)/shard_map/step/pallas_call | solution.py:326
  59.7 2.7 %write.1 = (f32[512,128]{1,0:T(8,128)}, f32[512,128]{1,0:T(8,128)}, f32[512,128]{1,0:T(8,128)}, f32[128,512]{1,0:T(8,128)}, f32[128,512]{1,0:T(8,128)}, /*index=...) custom-call(f32[512,128]{1,0:T(8,128)S(1)} %get-tuple-element.16.refs_0_, ...), custom_call_target="tpu_custom_call" | custom-call | tf_op jit(solution)/shard_map/write/pallas_call | solution.py:338

commit v2 on v1

--- a/solution.py
+++ b/solution.py
@@ -11,6 +11,81 @@
 F32, BF16 = jnp.float32, jnp.bfloat16
 NZ = 8
 S = 2
+REDUCE, FINISH, NORM, GATHER = 0, 1, 2, 3
+ORDER = (
+    (0, 0, 4, 1, 0),
+    (0, 0, 4, 1, 1),
+    (0, 0, 3, 0, 0),
+    (0, 0, 3, 0, 1),
+    (0, 1, 4, 1, 0),
+    (0, 1, 4, 1, 1),
+    (0, 0, 3, 1, 0),
+    (0, 0, 3, 1, 1),
+    (0, 0, 2, 0, 0),
+    (0, 0, 2, 0, 1),
+    (0, 1, 3, 0, 0),
+    (0, 1, 3, 0, 1),
+    (0, 0, 2, 1, 0),
+    (0, 0, 2, 1, 1),
+    (0, 0, 1, 0, 0),
+    (0, 0, 1, 0, 1),
+    (0, 1, 3, 1, 0),
+    (0, 1, 3, 1, 1),
+    (0, 0, 1, 1, 0),
+    (0, 0, 1, 1, 1),
+    (0, 1, 2, 0, 0),
+    (0, 1, 2, 0, 1),
+    (0, 1, 2, 1, 0),
+    (0, 1, 2, 1, 1),
+    (1, 0, 0, 0, 0),
+    (0, 1, 1, 0, 0),
+    (0, 1, 1, 0, 1),
+    (0, 1, 1, 1, 0),
+    (0, 1, 1, 1, 1),
+    (2, 0, 0, 0, 0),
+    (3, 0, 1, 1, 0),
+    (3, 0, 1, 1, 1),
+    (3, 0, 1, 0, 0),
+    (3, 0, 1, 0, 1),
+    (1, 1, 0, 0, 0),
+    (3, 0, 2, 1, 0),
+    (3, 0, 2, 1, 1),
+    (3, 0, 2, 0, 0),
+    (3, 0, 2, 0, 1),
+    (2, 1, 0, 0, 0),
+    (3, 1, 1, 1, 0),
+    (3, 1, 1, 1, 1),
+    (3, 1, 1, 0, 0),
+    (3, 1, 1, 0, 1),
+    (3, 0, 3, 1, 0),
+    (3, 0, 3, 1, 1),
+    (3, 0, 3, 0, 0),
+    (3, 0, 3, 0, 1),
+    (3, 1, 2, 1, 0),
+    (3, 1, 2, 1, 1),
+    (3, 1, 2, 0, 0),
+    (3, 1, 2, 0, 1),
+    (3, 0, 4, 1, 0),
+    (3, 0, 4, 1, 1),
+    (3, 0, 4, 0, 0),
+    (3, 0, 4, 0, 1),
+    (3, 1, 3, 1, 0),
+    (3, 1, 3, 1, 1),
+    (3, 1, 3, 0, 0),
+    (3, 1, 3, 0, 1),
+    (3, 0, 5, 1, 0),
+    (3, 0, 5, 1, 1),
+    (3, 1, 4, 1, 0),
+    (3, 1, 4, 1, 1),
+    (3, 1, 4, 0, 0),
+    (3, 1, 4, 0, 1),
+    (3, 1, 5, 1, 0),
+    (3, 1, 5, 1, 1),
+)
+SEMS = [
+    pltpu.SemaphoreType.DMA(shape)
+    for shape in ((2, NZ), (2, NZ), (2, 3), (2, NZ), (2, 14, S), (2, 14, S)) + ((2,),) * 7
+]
 UP, DOWN = 0, 1
 RIGHT, LEFT = 0, 1
 A, B = 0, 1
@@ -28,25 +103,34 @@
     return (moved, new_moment, new_second)
 
 
+def unit(way, half, hop):
+    return way * 7 + (hop - 1) * 2 + (half if hop <= 3 else 0)
+
+
 def reaches(way, half, hop):
     return hop <= 3 or (hop == 4 and half == way)
 
 
 def step_kernel(*refs):
+    def scoped(*sems):
+        step_body(*refs, *sems)
+
+    pl.run_scoped(scoped, *SEMS)
+
+
+def step_body(*refs):
     grads, state = refs[:2], (refs[2:5], refs[5:8])
     outs = (refs[8:11], refs[11:14])
     weights = refs[14:16]
     it = iter(refs[16:])
-    own, par = (next(it), next(it)), (next(it), next(it))
+    own, away, par = tuple((next(it), next(it)) for _ in range(3))
     snd, rcv = (next(it), next(it)), (next(it), next(it))
-    held = (tuple(next(it) for _ in range(3)), tuple(next(it) for _ in range(3)))
+    held = next(it), next(it)
     ex_s, ex_r, sq, scale = next(it), next(it), next(it), next(it)
-    own_sem, state_sem = next(it), next(it)
-    par_ss, par_rs = next(it), next(it)
-    rs_ss, rs_rs = next(it), next(it)
-    ag_ss, ag_rs = next(it), next(it)
-    cp_ss, cp_rs = next(it), next(it)
-    ex_ss, ex_rs = next(it), next(it)
+    own_sem, away_sem, state_sem = next(it), next(it), next(it)
+    par_rs, rs_rs, ag_rs = next(it), next(it), next(it)
+    cp_rs, ex_rs = next(it), next(it)
+    par_ss, rs_ss, ag_ss, cp_ss, ex_ss = tuple(next(it) for _ in range(5))
 
     dp, row, col = lax.axis_index("dp"), lax.axis_index("row"), lax.axis_index("col")
     z, core = dp // 2, dp % 2
@@ -66,10 +150,18 @@
             return grads[t].at[0, :, pl.ds(at, 128)]
         return grads[t].at[0, pl.ds(at, 128), :]
 
+    barrier = pltpu.get_barrier_semaphore()
+    for device in (partner, *beside, *peers):
+        pl.semaphore_signal(barrier, inc=1, device_id=device, device_id_type=MESH)
+
     order = (4, 3, 5, 2, 6, 1, 7, 0)
-    own_cp, par_cp = {}, {}
+    own_cp, away_cp, par_cp = {}, {}, {}
     for r in order:
         for t in (UP, DOWN):
+            away_cp[t, r] = pltpu.make_async_copy(
+                grad_block(t, r, 1 - core), away[t].at[r], away_sem.at[t, r]
+            )
+            away_cp[t, r].start()
             own_cp[t, r] = pltpu.make_async_copy(
                 grad_block(t, r, core), own[t].at[r], own_sem.at[t, r]
             )
@@ -77,28 +169,25 @@
     state_cp = {}
     for t in (UP, DOWN):
         for k in range(3):
-            state_cp[t, k] = pltpu.make_async_copy(state[t][k], held[t][k], state_sem.at[t, k])
+            state_cp[t, k] = pltpu.make_async_copy(state[t][k], held[t].at[k], state_sem.at[t, k])
             state_cp[t, k].start()
-
-    barrier = pltpu.get_barrier_semaphore()
-    for device in (partner, *beside, *peers):
-        pl.semaphore_signal(barrier, inc=1, device_id=device, device_id_type=MESH)
-    pl.semaphore_wait(barrier, 6)
-
-    sent = []
 
     def send(src, dst, ss, rs, to):
         copy = pltpu.make_async_remote_copy(
             src_ref=src, dst_ref=dst, send_sem=ss, recv_sem=rs, device_id=to, device_id_type=MESH
         )
         copy.start()
-        sent.append(copy)
         return copy
 
+    def took(ref, sem):
+        pltpu.make_async_copy(ref, ref, sem).wait()
+
+    pl.semaphore_wait(barrier, 6)
     for r in order:
         for t in (UP, DOWN):
+            away_cp[t, r].wait()
             par_cp[t, r] = send(
-                grad_block(t, r, 1 - core), par[t].at[r], par_ss.at[t, r], par_rs.at[t, r], partner
+                away[t].at[r], par[t].at[r], par_ss.at[t], par_rs.at[t, r], partner
             )
 
     def rows_of(t, half, s):
@@ -121,23 +210,12 @@
         total = chip_sum(t, hop if way == RIGHT else NZ - hop, half, s)
         if reaches(way, half, hop + 1):
             rs_cp[t, way, half, hop + 1, s].wait_recv()
-            total += rcv[t][way, half, hop, s].astype(F32)
-        snd[t][way, half, hop - 1, s] = total.astype(BF16)
+            total += rcv[t][unit(way, half, hop + 1), s].astype(F32)
+        u = unit(way, half, hop)
+        snd[t][u, s] = total.astype(BF16)
         rs_cp[t, way, half, hop, s] = send(
-            snd[t].at[way, half, hop - 1, s],
-            rcv[t].at[way, half, hop - 1, s],
-            rs_ss.at[t, way, half, hop - 1, s],
-            rs_rs.at[t, way, half, hop - 1, s],
-            beside[way],
+            snd[t].at[u, s], rcv[t].at[u, s], rs_ss.at[t], rs_rs.at[t, u, s], beside[way]
         )
-
-    def reduce_pair(t, which):
-        hop, far = which
-        for s in range(S):
-            for way in (RIGHT, LEFT):
-                reduce_hop(t, way, way if far else 1 - way, hop, s)
-
-    ex_cp = {}
 
     def finish_sum(t):
         for k in range(3):
@@ -154,9 +232,10 @@
                     at = pl.ds((half * S + s) * n + i, step)
                     grad = own[t][0, at, :].astype(F32) + par[t][0, at, :].astype(F32)
                     for way in (RIGHT, LEFT):
-                        grad += rcv[t][way, half, 0, s, pl.ds(i, step), :].astype(F32)
+                        u = unit(way, half, 1)
+                        grad += rcv[t][u, s, pl.ds(i, step), :].astype(F32)
                     moved, mom, sec = adam_move(
-                        held[t][0][at, :], held[t][1][at, :], held[t][2][at, :], grad * (1.0 / 16.0)
+                        held[t][0, at, :], held[t][1, at, :], held[t][2, at, :], grad * (1.0 / 16.0)
                     )
                     outs[t][0][at, :] = moved
                     outs[t][1][at, :] = mom
@@ -175,7 +254,7 @@
             acc = sq[...].T.reshape(16, 8, 128).sum(axis=0)
         ex_s[t] = acc
         for j, peer in enumerate(peers):
-            ex_cp[t, j] = send(ex_s.at[t], ex_r.at[t, j], ex_ss.at[t, j], ex_rs.at[t, j], peer)
+            send(ex_s.at[t], ex_r.at[t, j], ex_ss.at[t], ex_rs.at[t], peer)
 
     def slot(t, owner, half, s):
         n = PIECE[t][0]
@@ -184,8 +263,7 @@
         return weights[t].at[pl.ds(pl.multiple_of(owner * 128 + (half * S + s) * n, n), n), :]
 
     def renormalize(t):
-        for j in range(3):
-            ex_cp[t, j].wait_recv()
+        took(ex_r.at[t], ex_rs.at[t])
         total = ex_s[t] + ex_r[t, 0] + ex_r[t, 1] + ex_r[t, 2]
         factor = lax.rsqrt(total.sum(axis=0, keepdims=True) / D + 1e-06)
         rows = OPT[t][0]
@@ -203,11 +281,11 @@
                 outs[t][0][pl.ds(i, 16), :] = norm
                 weights[t][pl.ds(pl.multiple_of(at0 + i, 16), 16), :] = norm.astype(BF16)
 
-    ag_cp, copies = {}, []
-
-    def to_partner(t, owner, half, s, n):
+    ag_cp = {}
+
+    def to_partner(t, owner, half, s):
         at = slot(t, owner, half, s)
-        copies.append(send(at, at, cp_ss.at[t, n, s], cp_rs.at[t, n, s], partner))
+        send(at, at, cp_ss.at[t], cp_rs.at[t], partner)
 
     def gather_hop(t, way, half, hop, s):
         back = NZ - (hop - 1) if way == RIGHT else hop - 1
@@ -219,62 +297,36 @@
             ag_cp[t, way, half, hop, s] = send(
                 at,
                 at,
-                ag_ss.at[t, way, half, hop - 1, s],
-                ag_rs.at[t, way, half, hop - 1, s],
+                ag_ss.at[t],
+                ag_rs.at[t, unit(way, half, hop), s],
                 beside[way],
             )
         if hop > 1:
-            n = 2 + (way * 2 + half) * 4 + hop - 2
-            to_partner(t, owner, half, s, n)
-
-    def gather_level(t, hop):
-        for half in (0, 1):
-            for s in range(S):
-                for way in (RIGHT, LEFT):
-                    h = way if half == 0 else 1 - way
-                    if hop == 1 or reaches(way, h, hop - 1):
-                        gather_hop(t, way, h, hop, s)
-        if hop == 1:
-            for half in (A, B):
-                for s in range(S):
-                    to_partner(t, dp, half, s, half)
-
-    far, near = True, False
-    for t, hop, side in (
-        (UP, 4, far),
-        (UP, 3, near),
-        (DOWN, 4, far),
-        (UP, 3, far),
-        (UP, 2, near),
-        (DOWN, 3, near),
-        (UP, 2, far),
-        (UP, 1, near),
-        (DOWN, 3, far),
-        (UP, 1, far),
-        (DOWN, 2, near),
-        (DOWN, 2, far),
-    ):
-        reduce_pair(t, (hop, side))
-    finish_sum(UP)
-    reduce_pair(DOWN, (1, near))
-    reduce_pair(DOWN, (1, far))
-    renormalize(UP)
-    gather_level(UP, 1)
-    finish_sum(DOWN)
-    gather_level(UP, 2)
-    renormalize(DOWN)
-    gather_level(DOWN, 1)
-    gather_level(UP, 3)
-    gather_level(DOWN, 2)
-    gather_level(UP, 4)
-    gather_level(DOWN, 3)
-    gather_level(UP, 5)
-    gather_level(DOWN, 4)
-    gather_level(DOWN, 5)
-    for copy in copies:
-        copy.wait_recv()
-    for copy in sent:
-        copy.wait_send()
+            to_partner(t, owner, half, s)
+
+    for kind, t, hop, far, s in ORDER:
+        if kind == REDUCE:
+            for way in (RIGHT, LEFT):
+                reduce_hop(t, way, way if far else 1 - way, hop, s)
+        elif kind == FINISH:
+            finish_sum(t)
+        elif kind == NORM:
+            renormalize(t)
+        else:
+            for way in (RIGHT, LEFT):
+                gather_hop(t, way, way if far else 1 - way, hop, s)
+            if hop == 1 and far:
+                for half in (A, B):
+                    to_partner(t, dp, half, s)
+
+    for t in (UP, DOWN):
+        part = 1 if t == UP else BLOCK[t][0]
+        took(weights[t].at[pl.ds(0, 8 * part)], cp_rs.at[t])
+        took(weights[t].at[pl.ds(0, 8 * part)], cp_ss.at[t])
+        took(weights[t].at[pl.ds(0, 7 * part)], ag_ss.at[t])
+        took(snd[t], rs_ss.at[t])
+        took(par[t], par_ss.at[t])
+        took(ex_r.at[t], ex_ss.at[t])
 
 
 def write_kernel(*refs):
@@ -298,29 +350,16 @@
     mid = opt + [((2 * NZ, 512, 128), BF16), ((2048, 512), BF16)]
     out = opt + [((512, 2048), BF16), ((2048, 512), BF16)]
     dma = pltpu.SemaphoreType.DMA
+    both = (UP, DOWN)
     scratch = (
-        [pltpu.VMEM((NZ, *BLOCK[t]), BF16) for t in (UP, DOWN)]
-        + [pltpu.VMEM((NZ, *BLOCK[t]), BF16) for t in (UP, DOWN)]
-        + [pltpu.VMEM((2, 2, 4, S, *PIECE[t]), BF16) for t in (UP, DOWN)]
-        + [pltpu.VMEM((2, 2, 4, S, *PIECE[t]), BF16) for t in (UP, DOWN)]
-        + [pltpu.VMEM(OPT[t], F32) for t in (UP, DOWN) for _ in range(3)]
+        [pltpu.VMEM((NZ, *BLOCK[t]), BF16) for _ in range(3) for t in both]
+        + [pltpu.VMEM((14, S, *PIECE[t]), BF16) for _ in range(2) for t in both]
+        + [pltpu.VMEM((3, *OPT[t]), F32) for t in both]
         + [
             pltpu.VMEM((2, 8, 128), F32),
             pltpu.VMEM((2, 3, 8, 128), F32),
             pltpu.VMEM((128, 128), F32),
             pltpu.VMEM((128, 128), F32),
-            dma((2, NZ)),
-            dma((2, 3)),
-            dma((2, NZ)),
-            dma((2, NZ)),
-            dma((2, 2, 2, 4, S)),
-            dma((2, 2, 2, 4, S)),
-            dma((2, 2, 2, 4, S)),
-            dma((2, 2, 2, 4, S)),
-            dma((2, 18, S)),
-            dma((2, 18, S)),
-            dma((2, 3)),
-            dma((2, 3)),
         ]
     )
     mids = pl.pallas_call(

time: 62.5 us -> 57.8 us (0.925)
  Pallas kernels: 61.7 us -> 57.1 us
    pallas_call x1, Pallas kernels: 59.1 us -> 54.4 us  [on_device(): pl.pallas_call(step_kernel, out_shape=[pltpu.VMEM(shape, kind) for shape,...]
where the time goes in v2:
time: 57.8 us; the launch traced here: 57.7 us
  Pallas kernels  57.1 us (99%)
  between operations  0.64 us (1%)
    pallas_call x1, Pallas kernels, on_device(): pl.pallas_call(step_kernel, out_shape=[pltpu.VMEM(shape, kind) for shape,...  54.4 us
    pallas_call x1, Pallas kernels, on_device(): pl.pallas_call(write_kernel, out_shape=[jax.ShapeDtypeStruct(shape, kind)...  2.67 us

profile of v2, /device:TPU:1, one launch (start us, length us, event | category | flops | bytes accessed | tf_op | source)
XLA Modules:
  0.0 57.7 jit_solution(6032066094084352443)
XLA Ops:
  0.6 54.4 %step.1 = (f32[512,128]{1,0:T(8,128)S(1)}, f32[512,128]{1,0:T(8,128)S(1)}, f32[512,128]{1,0:T(8,128)S(1)}, f32[128,512]{1,0:T(8,128)S(1)}, f32[128,512]{1,0:T(8,...) custom-call(bf16[1,512,2048]{2,1,0:T(8,128)(2,1)} %refs_0_.1, ...), custom_call_target="tpu_custom_call" | custom-call | tf_op jit(solution)/shard_map/step/pallas_call | solution.py:365
  55.0 2.7 %write.1 = (f32[512,128]{1,0:T(8,128)}, f32[512,128]{1,0:T(8,128)}, f32[512,128]{1,0:T(8,128)}, f32[128,512]{1,0:T(8,128)}, f32[128,512]{1,0:T(8,128)}, /*index=...) custom-call(f32[512,128]{1,0:T(8,128)S(1)} %get-tuple-element.16.refs_0_, ...), custom_call_target="tpu_custom_call" | custom-call | tf_op jit(solution)/shard_map/write/pallas_call | solution.py:377
